TPU v7x, 256 devices: a whole 4x4x8 slice. The times are simulated.
256 devices in a mesh: tm: 8 (over x, y_lo), space: 32 (over y_hi, z, core).
Axes of the slice: x: 4, y: 4 (y_hi: 2, y_lo: 2; y = y_hi * 2 + y_lo), z: 8, core: 2. Of those that a mesh axis runs over, the one named last changes fastest.
Arguments:
- state: float32 [8, 6, 8, 512, 128], P('tm', None, None, 'space'), may hold values from -6 to 6
- multiplier: float32 [8, 6, 8, 512, 128], P('tm', None, None, 'space'), may hold values from -6 to 6
- members: bfloat16 [8, 40, 6, 8, 512, 128], P('tm', None, None, None, 'space'), may hold values from -6 to 6
- static_var: float32 [8, 6, 8, 512, 128], P('tm', None, None, 'space'), may hold values from 0.1 to 1
- courant: float32 [8, 2, 8, 512, 128], P('tm', None, None, 'space'), may hold values from -0.45 to 0.45
- coupling: float32 [8, 6, 6], replicated, may hold values from -2 to 2
- loc_offsets: int32 [9], replicated, may hold values from -8 to 8, as said below
Outputs:
- first_row: float32 [8, 6, 8, 512, 128], P('tm', None, None, 'space')
Inputs may be any that keep to these rules, and one draw needn't show every extreme that they name: `loc_offsets`: both -8 and 8 occur among the offsets.
All inputs are finite; a program needn't handle non-finite values.
Results may differ from a plain program's by a relative error of at most 0.0013.
Values may be sent and summed in bfloat16 or wider, within the bound.
A program may use at most 128 MiB of HBM per device.

v0:
```python
import jax
import jax.numpy as jnp
from jax import lax
from jax.sharding import PartitionSpec as P


def passed_along(block, axis, distance):
    devices = range(lax.axis_size(axis))
    route = [(i - distance, i) for i in devices if i - distance in devices]
    return lax.ppermute(block, axis, route)


def padded_2(array, sides, width):
    for axis, dim in sides:
        size, length = (lax.axis_size(axis), array.shape[dim])
        up = [(i, (i + 1) % size) for i in range(size)]
        down = [(j, i) for i, j in up]
        last = lax.slice_in_dim(array, length - width, length, axis=dim)
        leading = lax.slice_in_dim(array, 0, width, axis=dim)
        before = lax.ppermute(last, axis, up)
        after = lax.ppermute(leading, axis, down)
        array = jnp.concatenate([before, array, after], axis=dim)
    return array


def tangent_step(padded, winds, coupling):
    center = padded[:, :, 1:-1]
    west_cells = padded[:, :, :-2]
    east_cells = padded[:, :, 2:]
    zero_row = jnp.zeros_like(center[..., :1])
    south_cells = jnp.concatenate([zero_row, center[..., :-1]], axis=-1)
    north_cells = jnp.concatenate([center[..., 1:], zero_row], axis=-1)
    courant_x = winds[0]
    courant_y = winds[1]
    advection = jnp.maximum(courant_x, 0.0) * (center - west_cells)
    advection = advection + jnp.minimum(courant_x, 0.0) * (east_cells - center)
    advection = advection + jnp.maximum(courant_y, 0.0) * (center - south_cells)
    advection = advection + jnp.minimum(courant_y, 0.0) * (north_cells - center)
    coupling_term = jnp.einsum("lvw,wlxy->vlxy", coupling, center, precision=lax.Precision.HIGHEST)
    return center - advection + coupling_term


def per_device(state, multiplier, members, static_var, courant, coupling, loc_offsets):
    own_state = state[0]
    lagrange = multiplier[0]
    ensemble = members[0]
    variance = static_var[0]
    own_winds = courant[0]
    span_cells = ensemble.shape[3]
    radius = span_cells // 2
    member_count = ensemble.shape[0]
    stencil_count = loc_offsets.shape[0]
    weights = jnp.exp(-0.5 * (loc_offsets.astype(jnp.float32) / radius) ** 2)
    earlier = passed_along(own_state, "tm", 1)
    padded_state = padded_2(earlier, (("space", 2),), 2)
    padded_winds = padded_2(own_winds.astype(jnp.bfloat16), (("space", 2),), 1).astype(
        own_winds.dtype
    )
    halfway = tangent_step(padded_state, padded_winds, coupling)
    propagated = tangent_step(halfway, own_winds, coupling)
    products = (ensemble.astype(jnp.float32) * lagrange[None]).astype(jnp.bfloat16)
    padded_products = padded_2(products, (("space", 3),), radius)
    smoothed = jnp.zeros(ensemble.shape, jnp.float32)
    for index in range(stencil_count):
        offset_start = radius + loc_offsets[index]
        shifted = lax.dynamic_slice_in_dim(padded_products, offset_start, span_cells, 3)
        smoothed = smoothed + weights[index] * shifted.astype(jnp.float32)
    total = jnp.sum(ensemble.astype(jnp.float32) * smoothed, axis=0)
    localized = total / (member_count - 1)
    result = 0.5 * variance * lagrange + 0.5 * localized + own_state - propagated
    return result[None]


def solution(mesh):
    return jax.shard_map(
        per_device,
        mesh=mesh,
        in_specs=(
            P("tm", None, None, "space", None),
            P("tm", None, None, "space", None),
            P("tm", None, None, None, "space", None),
            P("tm", None, None, "space", None),
            P("tm", None, None, "space", None),
            P(),
            P(),
        ),
        out_specs=P("tm", None, None, "space", None),
        check_vma=False,
    )
```

profile of v0, /device:TPU:8, one launch (start us, length us, event | category | flops | bytes accessed | tf_op | source)
XLA Modules:
  0.0 145.4 jit_solution(6517384473953880711)
XLA Ops:
  0.0 0.0 copy-start
  0.0 5.4 %fusion = bf16[40,6,8,16,128]{4,3,2,1,0:T(8,128)(2,1)S(1)} fusion(bf16[1,40,6,8,16,128]{5,4,3,2,1,0:T(8,128)(2,1)} %param.9, f32[6,8,16,128]{3,2,1,0:T(8,128)} %bitcast.81), kind=kLoop, calls=%fused_computation.2 | loop fusion | flops 11796480 | bytes 16121856 | tf_op jit(solution)/shard_map/convert_element_type | solution.py:61
  5.4 0.0 copy-start.1
  5.4 3.0 %copy-done.1 = bf16[40,6,8,16,128]{4,3,2,1,0:T(8,128)(2,1)} copy-done((bf16[40,6,8,16,128]{4,3,2,1,0:T(8,128)(2,1)}, bf16[40,6,8,16,128]{4,3,2,1,0:T(8,128)(2,1)S(1)}, u32[]{:S(2)}) %copy-start.1) | copy-done | bytes 7864344
  8.5 4.1 %fusion.26 = (bf16[40,6,8,8,128]{4,3,2,1,0:T(8,128)(2,1)}, bf16[40,6,8,8,128]{4,3,2,1,0:T(8,128)(2,1)}) fusion(bf16[40,6,8,16,128]{4,3,2,1,0:T(8,128)(2,1)S(1)} %fusion), kind=kLoop, calls=%fused_computation.49 | loop fusion | bytes 15728640 | tf_op jit(solution)/shard_map/slice | solution.py:18
  12.5 0.0 collective-permute-start
  12.5 7.0 %collective-permute-start.1 = (bf16[40,6,8,8,128]{4,3,2,1,0:T(8,128)(2,1)}, bf16[40,6,8,8,128]{4,3,2,1,0:T(8,128)(2,1)}, u32[]{:S(2)}, u32[]{:S(2)}) collective-permute-start(bf16[40,6,8,8,128]{4,3,2,1,0:T(8,128)(2,1)} %get-tuple-element.6), channel_id=1, source_target_pairs={{1,0},{2,1},{3,2},{4,3},{5,4},{6,5},{7,6},{8,7},{9,8},{10,9},{11,1... | collective-permute-start | bytes 11796488 | tf_op jit(solution)/shard_map/ppermute | solution.py:21
  19.5 0.2 copy.48
  19.8 4.2 %collective-permute-start.2 = (f32[6,8,16,128]{3,0,2,1:T(8,128)S(1)}, f32[6,8,16,128]{3,0,2,1:T(8,128)S(1)}, u32[]{:S(2)}, u32[]{:S(2)}) collective-permute-start(f32[6,8,16,128]{3,0,2,1:T(8,128)S(1)} %bitcast.82), channel_id=1, source_target_pairs={{0,32},{32,64},{64,96},{96,128},{128,160},{160,192},{192,224},{1,3... | collective-permute-start | bytes 1179656 | tf_op jit(solution)/shard_map/ppermute | solution.py:10
  24.0 0.1 collective-permute-start.5
  24.1 5.3 %collective-permute-start.6 = (bf16[2,8,1,128]{3,2,1,0:T(2,128)(2,1)S(1)}, bf16[2,8,1,128]{3,2,1,0:T(2,128)(2,1)S(1)}, u32[]{:S(2)}, u32[]{:S(2)}) collective-permute-start(bf16[2,8,1,128]{3,2,1,0:T(2,128)(2,1)S(1)} %get-tuple-element.22), channel_id=1, source_target_pairs={{1,0},{2,1},{3,2},{4,3},{5,4},{6,5},{7,6},{8,7},{9,8},{10,9},{11,1... | collective-permute-start | bytes 12296 | tf_op jit(solution)/shard_map/ppermute | solution.py:21
  29.5 0.7 maximum_bitcast_fusion.3
  30.1 0.0 copy-done.6
  30.2 0.7 fusion.32
  30.8 0.7 fusion.31
  42.9 20.3 %collective-permute-done.5 = bf16[2,8,1,128]{3,2,1,0:T(2,128)(2,1)S(1)} collective-permute-done((bf16[2,8,1,128]{3,2,1,0:T(2,128)(2,1)S(1)}, bf16[2,8,1,128]{3,2,1,0:T(2,128)(2,1)S(1)}, u32[]{:S(2)}, u32[]{:S(2)}) %collective-permute-start.5) | collective-permute-done | bytes 4128 | tf_op jit(solution)/shard_map/ppermute | solution.py:20
  63.2 0.0 collective-permute-done.6
  63.3 9.5 %collective-permute-done.2 = f32[6,8,16,128]{3,0,2,1:T(8,128)S(1)} collective-permute-done((f32[6,8,16,128]{3,0,2,1:T(8,128)S(1)}, f32[6,8,16,128]{3,0,2,1:T(8,128)S(1)}, u32[]{:S(2)}, u32[]{:S(2)}) %collective-permute-start.2) | collective-permute-done | bytes 393248 | tf_op jit(solution)/shard_map/ppermute | solution.py:10
  72.7 0.1 collective-permute-start.3
  72.9 5.6 %collective-permute-start.4 = (f32[6,8,2,128]{3,0,2,1:T(8,128)S(1)}, f32[6,8,2,128]{3,0,2,1:T(8,128)S(1)}, u32[]{:S(2)}, u32[]{:S(2)}) collective-permute-start(f32[6,8,2,128]{3,0,2,1:T(8,128)S(1)} %get-tuple-element.11), channel_id=1, source_target_pairs={{1,0},{2,1},{3,2},{4,3},{5,4},{6,5},{7,6},{8,7},{9,8},{10,9},{11,1... | collective-permute-start | bytes 147464 | tf_op jit(solution)/shard_map/ppermute | solution.py:21
  78.5 1.7 %collective-permute-done.3 = f32[6,8,2,128]{3,0,2,1:T(8,128)S(1)} collective-permute-done((f32[6,8,2,128]{3,0,2,1:T(8,128)S(1)}, f32[6,8,2,128]{3,0,2,1:T(8,128)S(1)}, u32[]{:S(2)}, u32[]{:S(2)}) %collective-permute-start.3) | collective-permute-done | bytes 49184 | tf_op jit(solution)/shard_map/ppermute | solution.py:20
  80.2 0.2 collective-permute-done.4
  80.4 0.2 fusion.27
  80.6 0.0 copy-done
  80.6 1.0 fusion.7
  81.6 0.2 fusion.28
  81.8 0.0 collective-permute-done
  81.8 0.0 collective-permute-done.1
  81.9 10.7 %pad_maximum_fusion = bf16[40,6,8,32,128]{4,3,2,1,0:T(8,128)(2,1)} fusion(bf16[40,6,8,8,128]{4,3,2,1,0:T(8,128)(2,1)} %collective-permute-done.1, bf16[40,6,8,16,128]{4,3,2,1,0:T(8,128)(2,1)S(1)} %copy-done.2, bf16[40,6,8,8,128]{4,3,2,1,0:T(8,128)(2,1)} %collective-permute-done), kind=kLoop, calls=%fused_computation.4 | loop fusion | flops 47185920 | bytes 31457280 | tf_op jit(solution)/shard_map/concatenate | solution.py:22
  92.5 49.2 %fusion.1 = f32[6,8,16,128]{3,2,1,0:T(8,128)S(1)} fusion(bf16[1,40,6,8,16,128]{5,4,3,2,1,0:T(8,128)(2,1)} %param.9, bf16[40,6,8,32,128]{4,3,2,1,0:T(8,128)(2,1)} %pad_maximum_fusion, s32[]{:T(128)S(6)} %select_n.35, f32[]{:T(128)} %bitcast.29, s32[]{:T(128)S(6)} %select_n.34, f32[]{:T(128)} %bitcast.26, s32[]{:T(128)S(6)} %select_n.33, f32[]{:T(128)} %bitcast.23, ...), kind=kLoop, calls=%fused_computation.3 | loop fusion | flops 113934336 | bytes 79036488 | tf_op jit(solution)/shard_map/reduce_sum | solution.py:68
  141.8 2.8 %fusion.16 = f32[1,6,8,16,128]{4,1,3,2,0:T(8,128)S(1)} fusion(f32[6,8,18,128]{3,0,2,1:T(8,128)S(1)} %fusion.7, f32[6,8,16,128]{3,2,1,0:T(8,128)S(1)} %fusion.1, f32[1,6,8,16,128]{4,3,2,1,0:T(8,128)S(1)} %copy-done.4, f32[1,6,8,16,128]{4,3,2,1,0:T(8,128)} %param.10, f32[6,8,16,127]{3,0,2,1:T(8,128)S(1)} %get-tuple-element.10, ...), kind=kOutput, calls=%fused_computation.24 | convolution fusion | flops 8945664 | bytes 5464064 | tf_op jit(solution)/shard_map/lvw,wlxy->vlxy/dot_general | solution.py:39
  144.6 0.8 copy.22
  (18 shorter events, 0.2 us)
Async XLA Ops:
  0.0 80.6 %copy-start = (f32[8,6,6]{2,0,1:T(8,128)S(1)}, f32[8,6,6]{2,0,1:T(8,128)}, u32[]{:S(2)}) copy-start(f32[8,6,6]{2,0,1:T(8,128)} %param.12) | copy-start | bytes 3460
  0.0 19.5 %copy-start.3 = (f32[1,6,8,16,128]{4,3,2,1,0:T(8,128)S(1)}, f32[1,6,8,16,128]{4,3,2,1,0:T(8,128)}, u32[]{:S(2)}) copy-start(f32[1,6,8,16,128]{4,3,2,1,0:T(8,128)} %param.7) | copy-start | bytes 1179652
  0.0 30.1 %copy-start.6 = (s32[9]{0:T(128)S(1)}, s32[9]{0:T(128)}, u32[]{:S(2)}) copy-start(s32[9]{0:T(128)} %param.13) | copy-start | bytes 112
  5.4 3.0 %copy-start.1 = (bf16[40,6,8,16,128]{4,3,2,1,0:T(8,128)(2,1)}, bf16[40,6,8,16,128]{4,3,2,1,0:T(8,128)(2,1)S(1)}, u32[]{:S(2)}) copy-start(bf16[40,6,8,16,128]{4,3,2,1,0:T(8,128)(2,1)S(1)} %fusion) | copy-start | bytes 23592964
  8.5 15.5 %copy-start.5 = (f32[1,2,8,16,128]{4,3,2,1,0:T(8,128)S(1)}, f32[1,2,8,16,128]{4,3,2,1,0:T(8,128)}, u32[]{:S(2)}) copy-start(f32[1,2,8,16,128]{4,3,2,1,0:T(8,128)} %param.11) | copy-start | bytes 393220
  12.5 69.3 %collective-permute-start = (bf16[40,6,8,8,128]{4,3,2,1,0:T(8,128)(2,1)}, bf16[40,6,8,8,128]{4,3,2,1,0:T(8,128)(2,1)}, u32[]{:S(2)}, u32[]{:S(2)}) collective-permute-start(bf16[40,6,8,8,128]{4,3,2,1,0:T(8,128)(2,1)} %get-tuple-element.5), channel_id=1, source_target_pairs={{0,1},{1,2},{2,3},{3,4},{4,5},{5,6},{6,7},{7,8},{8,9},{9,10},{10,1... | collective-permute-start | bytes 11796488 | tf_op jit(solution)/shard_map/ppermute | solution.py:20
  12.5 69.3 %collective-permute-start.1 = (bf16[40,6,8,8,128]{4,3,2,1,0:T(8,128)(2,1)}, bf16[40,6,8,8,128]{4,3,2,1,0:T(8,128)(2,1)}, u32[]{:S(2)}, u32[]{:S(2)}) collective-permute-start(bf16[40,6,8,8,128]{4,3,2,1,0:T(8,128)(2,1)} %get-tuple-element.6), channel_id=1, source_target_pairs={{1,0},{2,1},{3,2},{4,3},{5,4},{6,5},{7,6},{8,7},{9,8},{10,9},{11,1... | collective-permute-start | bytes 11796488 | tf_op jit(solution)/shard_map/ppermute | solution.py:21
  19.8 52.9 %collective-permute-start.2 = (f32[6,8,16,128]{3,0,2,1:T(8,128)S(1)}, f32[6,8,16,128]{3,0,2,1:T(8,128)S(1)}, u32[]{:S(2)}, u32[]{:S(2)}) collective-permute-start(f32[6,8,16,128]{3,0,2,1:T(8,128)S(1)} %bitcast.82), channel_id=1, source_target_pairs={{0,32},{32,64},{64,96},{96,128},{128,160},{160,192},{192,224},{1,3... | collective-permute-start | bytes 1179656 | tf_op jit(solution)/shard_map/ppermute | solution.py:10
  24.0 39.2 %collective-permute-start.5 = (bf16[2,8,1,128]{3,2,1,0:T(2,128)(2,1)S(1)}, bf16[2,8,1,128]{3,2,1,0:T(2,128)(2,1)S(1)}, u32[]{:S(2)}, u32[]{:S(2)}) collective-permute-start(bf16[2,8,1,128]{3,2,1,0:T(2,128)(2,1)S(1)} %get-tuple-element.21), channel_id=1, source_target_pairs={{0,1},{1,2},{2,3},{3,4},{4,5},{5,6},{6,7},{7,8},{8,9},{9,10},{10,1... | collective-permute-start | bytes 12296 | tf_op jit(solution)/shard_map/ppermute | solution.py:20
  24.1 39.1 %collective-permute-start.6 = (bf16[2,8,1,128]{3,2,1,0:T(2,128)(2,1)S(1)}, bf16[2,8,1,128]{3,2,1,0:T(2,128)(2,1)S(1)}, u32[]{:S(2)}, u32[]{:S(2)}) collective-permute-start(bf16[2,8,1,128]{3,2,1,0:T(2,128)(2,1)S(1)} %get-tuple-element.22), channel_id=1, source_target_pairs={{1,0},{2,1},{3,2},{4,3},{5,4},{6,5},{7,6},{8,7},{9,8},{10,9},{11,1... | collective-permute-start | bytes 12296 | tf_op jit(solution)/shard_map/ppermute | solution.py:21
  42.9 38.9 %copy-start.2 = (bf16[40,6,8,16,128]{4,3,2,1,0:T(8,128)(2,1)S(1)}, bf16[40,6,8,16,128]{4,3,2,1,0:T(8,128)(2,1)}, u32[]{:S(2)}) copy-start(bf16[40,6,8,16,128]{4,3,2,1,0:T(8,128)(2,1)} %copy-done.1) | copy-start | bytes 23592964
  72.7 7.4 %collective-permute-start.3 = (f32[6,8,2,128]{3,0,2,1:T(8,128)S(1)}, f32[6,8,2,128]{3,0,2,1:T(8,128)S(1)}, u32[]{:S(2)}, u32[]{:S(2)}) collective-permute-start(f32[6,8,2,128]{3,0,2,1:T(8,128)S(1)} %get-tuple-element.12), channel_id=1, source_target_pairs={{0,1},{1,2},{2,3},{3,4},{4,5},{5,6},{6,7},{7,8},{8,9},{9,10},{10,1... | collective-permute-start | bytes 147464 | tf_op jit(solution)/shard_map/ppermute | solution.py:20
  72.9 7.5 %collective-permute-start.4 = (f32[6,8,2,128]{3,0,2,1:T(8,128)S(1)}, f32[6,8,2,128]{3,0,2,1:T(8,128)S(1)}, u32[]{:S(2)}, u32[]{:S(2)}) collective-permute-start(f32[6,8,2,128]{3,0,2,1:T(8,128)S(1)} %get-tuple-element.11), channel_id=1, source_target_pairs={{1,0},{2,1},{3,2},{4,3},{5,4},{6,5},{7,6},{8,7},{9,8},{10,9},{11,1... | collective-permute-start | bytes 147464 | tf_op jit(solution)/shard_map/ppermute | solution.py:21
  92.5 49.2 %copy-start.4 = (f32[1,6,8,16,128]{4,3,2,1,0:T(8,128)S(1)}, f32[1,6,8,16,128]{4,3,2,1,0:T(8,128)}, u32[]{:S(2)}) copy-start(f32[1,6,8,16,128]{4,3,2,1,0:T(8,128)} %param.8) | copy-start | bytes 1179652
where the time goes:
time: 148 us; the launch traced here: 145 us
  other arithmetic  66.1 us (45%)
  waiting for transfers between devices  31.6 us (21%)
  starting transfers between devices  22.3 us (15%)
  between operations  11.5 us (8%)
  local copies, waits for them, and re-layouts  10.1 us (7%)
  matrix products  3.79 us (3%)
    reduce_sum x1, other arithmetic, per_device(): total = jnp.sum(ensemble.astype(jnp.float32) * smoothed, axis=0)  49.2 us
    ppermute x3, waiting for transfers between devices, padded_2(): before = lax.ppermute(last, axis, up)  22 us
    ppermute x3, starting transfers between devices, padded_2(): after = lax.ppermute(leading, axis, down)  18 us
    concatenate x1, other arithmetic, padded_2(): array = jnp.concatenate([before, array, after], axis=dim)  10.7 us
    ppermute x1, waiting for transfers between devices, passed_along(): return lax.ppermute(block, axis, route)  9.45 us
    convert_element_type x1, other arithmetic, per_device(): (ensemble.astype(jnp.float32) * lagrange[None]).astype(jnp.bfloat16)  5.38 us
    ppermute x1, starting transfers between devices, passed_along(): return lax.ppermute(block, axis, route)  4.18 us
    slice x2, local copies, waits for them, and re-layouts, padded_2(): last = lax.slice_in_dim(array, length - width, length, axis=dim)  4.07 us
  transfers between devices with their start and end apart: 7, of which 4 were waited for; matrix products, arithmetic and copies ran while one was open for 3% of the time, Pallas kernels for 0%

commit v1 on v0

v1 whole, which is shorter than its diff:
```python
import functools
import jax
import jax.numpy as jnp
from jax import lax
from jax.experimental import pallas as pl
from jax.experimental.pallas import tpu as pltpu
from jax.sharding import PartitionSpec as P

MESH = pl.DeviceIdType.MESH
GROUP = 10
RADIUS = 8
LEVELS_PER_CHUNK = 2


def column_of(index, width, side):
    own = GROUP * width
    in_halo = index >= own
    halo_index = index - own
    member = jnp.where(in_halo, halo_index >> 3, index >> 4)
    halo_column = (halo_index & 7) + jnp.where(side == 0, -RADIUS, width)
    column = jnp.where(in_halo, halo_column, index & (width - 1))
    return member, column, in_halo


def stencil_matrix(offsets, side, width, rows, row_start):
    size = GROUP * (width + RADIUS)
    shape = (rows, size)
    row = lax.broadcasted_iota(jnp.int32, shape, 0) + row_start
    col = lax.broadcasted_iota(jnp.int32, shape, 1)
    row_member, row_column, row_halo = column_of(row, width, side)
    col_member, col_column, col_halo = column_of(col, width, side)
    distance = col_column - row_column
    count = jnp.zeros(shape, jnp.float32)
    for j in range(offsets.shape[0]):
        count = count + jnp.where(distance == offsets[j], 1.0, 0.0)
    keep = (row_member == col_member) & ~(row_halo & col_halo)
    scaled = distance.astype(jnp.float32) * (1.0 / RADIUS)
    return jnp.where(keep, count * jnp.exp(-0.5 * scaled * scaled), 0.0)


def kernel(
    sizes,
    offsets,
    coupling,
    state_hbm,
    mult_hbm,
    mem_hbm,
    var_hbm,
    wind_hbm,
    out,
    own,
    halo,
    lam,
    lam_halo,
    state,
    prev,
    var,
    wind,
    state_edge,
    state_halo,
    wind_edge,
    wind_halo,
    total,
    base,
    back_out,
    back_in,
    stencil,
    local_sem,
    own_sem,
    mem_send,
    mem_recv,
    back_send,
    back_recv,
    lam_send,
    lam_recv,
    state_send,
    state_recv,
    edge_send,
    edge_recv,
    wind_send,
    wind_recv,
):
    n_tm, n_space = sizes
    members, n_var, n_lev, width, _ = own.shape
    half = n_var // 2
    per_var = n_lev // LEVELS_PER_CHUNK
    chunks = half * per_var
    t = lax.axis_index("tm")
    s = lax.axis_index("space")
    parity = lax.rem(s, 2)
    t_next, t_last = lax.rem(t + 1, n_tm), lax.rem(t + n_tm - 1, n_tm)
    s_next, s_last = lax.rem(s + 1, n_space), lax.rem(s + n_space - 1, n_space)

    barrier = pltpu.get_barrier_semaphore()
    for peer in ((t, s_next), (t, s_last), (t_last, s), (t_last, s_next), (t_last, s_last)):
        pl.semaphore_signal(barrier, inc=1, device_id=peer, device_id_type=MESH)

    load_state = pltpu.make_async_copy(state_hbm.at[0], state, local_sem.at[0])
    load_wind = pltpu.make_async_copy(
        wind_hbm.at[0], wind.at[:, :, pl.ds(8, width)], local_sem.at[1]
    )
    load_lam = pltpu.make_async_copy(mult_hbm.at[0], lam, local_sem.at[2])
    load_var = pltpu.make_async_copy(var_hbm.at[0], var, local_sem.at[3])
    load_state.start()
    load_wind.start()
    load_lam.start()
    load_var.start()

    def load_own(v):
        return pltpu.make_async_copy(mem_hbm.at[0, :, v], own.at[:, v], own_sem.at[v])

    def neighbour(side):
        return lax.rem(s + n_space - 1 + 2 * side, n_space)

    def send(src, dst, send_sem, recv_sem, where):
        return pltpu.make_async_remote_copy(
            src_ref=src,
            dst_ref=dst,
            send_sem=send_sem,
            recv_sem=recv_sem,
            device_id=where,
            device_id_type=MESH,
        )

    def mem_copy(h, k):
        v, level = k // per_var, lax.rem(k, per_var) * LEVELS_PER_CHUNK
        levels = pl.ds(level, LEVELS_PER_CHUNK)
        rows = pl.ds(pl.multiple_of((1 - h) * RADIUS, RADIUS), RADIUS)
        return send(
            mem_hbm.at[0, :, half * h + v, levels, rows],
            halo.at[h, :, v, levels],
            mem_send.at[h, k],
            mem_recv.at[h, k],
            (t, neighbour(1 - h)),
        )

    def lam_copy(h):
        rows = pl.ds((1 - h) * RADIUS, RADIUS)
        return send(
            mult_hbm.at[0, pl.ds(half * h, half), :, rows],
            lam_halo.at[h],
            lam_send.at[h],
            lam_recv.at[h],
            (t, neighbour(1 - h)),
        )

    def back_copy(h, k):
        v, level = k // per_var, lax.rem(k, per_var) * LEVELS_PER_CHUNK
        levels = pl.ds(level, LEVELS_PER_CHUNK)
        return send(
            back_out.at[h, v, levels],
            back_in.at[h, v, levels],
            back_send.at[h, k],
            back_recv.at[h, k],
            (t, neighbour(h)),
        )

    state_copy = send(
        state_hbm.at[0],
        prev.at[:, :, pl.ds(8, width)],
        state_send.at[0],
        state_recv.at[0],
        (t_next, s),
    )

    def edge_copy(h):
        return send(
            state_edge.at[h],
            state_halo.at[h],
            edge_send.at[h],
            edge_recv.at[h],
            (t_next, neighbour(1 - h)),
        )

    def wind_copy(h):
        return send(
            wind_edge.at[h],
            wind_halo.at[h],
            wind_send.at[h],
            wind_recv.at[h],
            (t, neighbour(1 - h)),
        )

    pl.semaphore_wait(barrier, 5)
    for h in range(2):
        lam_copy(h).start()
    for h in range(2):
        mem_copy(h, 0).start()
    state_copy.start()

    def start_members(k, carry):
        for h in range(2):
            mem_copy(h, k).start()
        return carry

    lax.fori_loop(1, chunks // 2, start_members, 0)

    def start_own(v, carry):
        d2d_side = 1 - parity
        load_own(lax.rem(v // 2 + half * lax.rem(d2d_side + lax.rem(v, 2), 2), n_var)).start()
        return carry

    lax.fori_loop(0, n_var, start_own, 0)

    load_state.wait()
    load_wind.wait()
    for c in range(2):
        state_edge[0, c] = state[:, :, width - 2 + c]
        state_edge[1, c] = state[:, :, c]
    wind_edge[0] = wind[:, :, 8 + width - 1]
    wind_edge[1] = wind[:, :, 8]

    size = GROUP * (width + RADIUS)
    block = 48

    def build(step, carry):
        side = step // (size // block)
        row_start = pl.multiple_of(lax.rem(step, size // block) * block, block)
        matrix = stencil_matrix(offsets, side, width, block, row_start)
        high = matrix.astype(jnp.bfloat16)
        stencil[side, 0, pl.ds(row_start, block)] = high
        stencil[side, 1, pl.ds(row_start, block)] = (matrix - high.astype(jnp.float32)).astype(
            jnp.bfloat16
        )
        return carry

    lax.fori_loop(0, 2 * (size // block), build, 0)
    for h in range(2):
        edge_copy(h).start()
        wind_copy(h).start()
    lax.fori_loop(chunks // 2, chunks, start_members, 0)
    load_lam.wait()

    def one_level(side, v, level):
        full_v = half * side + v
        lam_own = lam[full_v, level]
        lam_far = lam_halo[side, v, level]
        own_sum = jnp.zeros((width, 128), jnp.float32)
        far_sum = jnp.zeros((RADIUS, 128), jnp.float32)
        for pair in range(members // (2 * GROUP)):
            fields, products = [], []
            for q in (2 * pair, 2 * pair + 1):
                near = own[pl.ds(q * GROUP, GROUP), full_v, level].astype(jnp.float32)
                far = halo[side, pl.ds(q * GROUP, GROUP), v, level].astype(jnp.float32)
                fields.append((near, far))
                near = (near * lam_own[None]).reshape(GROUP * width, 128)
                far = (far * lam_far[None]).reshape(GROUP * RADIUS, 128)
                products.append(jnp.concatenate([near, far], axis=0).astype(jnp.bfloat16))
            rhs = jnp.concatenate(products, axis=1)
            smooth = jnp.dot(stencil[side, 0], rhs, preferred_element_type=jnp.float32)
            smooth = smooth + jnp.dot(stencil[side, 1], rhs, preferred_element_type=jnp.float32)
            for i, (near, far) in enumerate(fields):
                part = smooth[:, 128 * i : 128 * (i + 1)]
                own_part = part[: GROUP * width].reshape(GROUP, width, 128)
                far_part = part[GROUP * width :].reshape(GROUP, RADIUS, 128)
                own_sum = own_sum + jnp.sum(near * own_part, axis=0)
                far_sum = far_sum + jnp.sum(far * far_part, axis=0)
        total[full_v, level] = own_sum
        back_out[side, v, level] = far_sum

    def step(j, carry):
        k, over_ici = j // 2, lax.rem(j, 2)
        side = lax.rem(parity + 1 - over_ici, 2)
        v, level = k // per_var, lax.rem(k, per_var) * LEVELS_PER_CHUNK

        @pl.when(lax.rem(k, per_var) == 0)
        def _():
            load_own(half * side + v).wait()

        @pl.when(k == 0)
        def _():
            lam_copy_wait(side)

        mem_copy(side, k).wait_recv()

        def each(d, c):
            one_level(side, v, level + d)
            return c

        lax.fori_loop(0, LEVELS_PER_CHUNK, each, 0)
        back_copy(side, k).start()
        return carry

    def lam_copy_wait(h):
        send(
            mult_hbm.at[0, pl.ds(0, half), :, pl.ds(0, RADIUS)],
            lam_halo.at[h],
            lam_send.at[h],
            lam_recv.at[h],
            (t, neighbour(1 - h)),
        ).wait_recv()

    middle = 2 * ((3 * chunks) // 4)
    lax.fori_loop(0, middle, step, 0)

    state_copy.wait_recv()
    for h in range(2):
        edge_copy(h).wait_recv()
        wind_copy(h).wait_recv()
    load_var.wait()
    padded = width + 16
    rows = lax.broadcasted_iota(jnp.int32, (padded, 128), 0)
    lanes = lax.broadcasted_iota(jnp.int32, (padded, 128), 1)
    for c in range(2):
        prev[:, :, 6 + c] = state_halo[0, c]
        prev[:, :, 8 + width + c] = state_halo[1, c]
    wind[:, :, 7] = wind_halo[0]
    wind[:, :, 8 + width] = wind_halo[1]
    first = jnp.where(t == 0, 0.0, 1.0)

    def tangent(level, carry):
        inside = (rows >= 6) & (rows < 8 + width + 2)
        fields = [jnp.where(inside, prev[v, level], 0.0) for v in range(n_var)]
        wind_x = jnp.where(inside, wind[0, level], 0.0)
        wind_y = jnp.where(inside, wind[1, level], 0.0)
        x_up, x_down = jnp.maximum(wind_x, 0.0), jnp.minimum(wind_x, 0.0)
        y_up, y_down = jnp.maximum(wind_y, 0.0), jnp.minimum(wind_y, 0.0)
        for _ in range(2):
            new = []
            for v in range(n_var):
                f = fields[v]
                west = pltpu.roll(f, 1, 0)
                east = pltpu.roll(f, padded - 1, 0)
                south = jnp.where(lanes == 0, 0.0, pltpu.roll(f, 1, 1))
                north = jnp.where(lanes == 127, 0.0, pltpu.roll(f, 127, 1))
                moved = x_up * (f - west) + x_down * (east - f)
                moved = moved + y_up * (f - south) + y_down * (north - f)
                mixed = coupling[v, level, 0] * fields[0]
                for w in range(1, n_var):
                    mixed = mixed + coupling[v, level, w] * fields[w]
                new.append(f - moved + mixed)
            fields = new
        for v in range(n_var):
            propagated = jnp.where(first > 0.5, fields[v][8 : 8 + width], 0.0)
            base[v, level] = (
                0.5 * var[v, level] * lam[v, level] + state[v, level] - propagated
            )
        return carry

    lax.fori_loop(0, n_lev, tangent, 0)
    lax.fori_loop(middle, 2 * chunks, step, 0)

    def drain(k, carry):
        for h in range(2):
            back_copy(h, k).wait_recv()
            back_copy(h, k).wait_send()
            mem_copy(h, k).wait_send()
        return carry

    lax.fori_loop(0, chunks, drain, 0)
    scale = 0.5 / (members - 1)
    for h in range(2):
        for v in range(half):
            full_v = half * h + v
            lo, hi = (0, RADIUS) if h == 1 else (width - RADIUS, width)
            keep_lo, keep_hi = (RADIUS, width) if h == 1 else (0, width - RADIUS)
            out[0, full_v, :, lo:hi] = base[full_v, :, lo:hi] + scale * (
                total[full_v, :, lo:hi] + back_in[h, v]
            )
            out[0, full_v, :, keep_lo:keep_hi] = (
                base[full_v, :, keep_lo:keep_hi] + scale * total[full_v, :, keep_lo:keep_hi]
            )
    state_copy.wait_send()
    for h in range(2):
        lam_copy(h).wait_send()
        edge_copy(h).wait_send()
        wind_copy(h).wait_send()


def per_device(sizes, state, multiplier, members, static_var, courant, coupling, loc_offsets):
    _, n_mem, n_var, n_lev, width, lanes = members.shape
    half = n_var // 2
    chunks = half * (n_lev // LEVELS_PER_CHUNK)
    size = GROUP * (width + RADIUS)
    f32, bf16 = jnp.float32, jnp.bfloat16
    dma = pltpu.SemaphoreType.DMA
    hbm = pl.BlockSpec(memory_space=pl.ANY)
    smem = pl.BlockSpec(memory_space=pltpu.SMEM)
    return pl.pallas_call(
        functools.partial(kernel, sizes),
        out_shape=jax.ShapeDtypeStruct(state.shape, f32),
        in_specs=[smem, smem, hbm, hbm, hbm, hbm, hbm],
        out_specs=pl.BlockSpec(memory_space=pltpu.VMEM),
        scratch_shapes=[
            pltpu.VMEM((n_mem, n_var, n_lev, width, lanes), bf16),
            pltpu.VMEM((2, n_mem, half, n_lev, RADIUS, lanes), bf16),
            pltpu.VMEM((n_var, n_lev, width, lanes), f32),
            pltpu.VMEM((2, half, n_lev, RADIUS, lanes), f32),
            pltpu.VMEM((n_var, n_lev, width, lanes), f32),
            pltpu.VMEM((n_var, n_lev, width + 16, lanes), f32),
            pltpu.VMEM((n_var, n_lev, width, lanes), f32),
            pltpu.VMEM((2, n_lev, width + 16, lanes), f32),
            pltpu.VMEM((2, 2, n_var, n_lev, lanes), f32),
            pltpu.VMEM((2, 2, n_var, n_lev, lanes), f32),
            pltpu.VMEM((2, 2, n_lev, lanes), f32),
            pltpu.VMEM((2, 2, n_lev, lanes), f32),
            pltpu.VMEM((n_var, n_lev, width, lanes), f32),
            pltpu.VMEM((n_var, n_lev, width, lanes), f32),
            pltpu.VMEM((2, half, n_lev, RADIUS, lanes), f32),
            pltpu.VMEM((2, half, n_lev, RADIUS, lanes), f32),
            pltpu.VMEM((2, 2, size, size), bf16),
            dma((4,)),
            dma((n_var,)),
            dma((2, chunks)),
            dma((2, chunks)),
            dma((2, chunks)),
            dma((2, chunks)),
            dma((2,)),
            dma((2,)),
            dma((1,)),
            dma((1,)),
            dma((2,)),
            dma((2,)),
            dma((2,)),
            dma((2,)),
        ],
        compiler_params=pltpu.CompilerParams(
            collective_id=0, has_side_effects=True, vmem_limit_bytes=67043328
        ),
        name="hybrid_row",
    )(loc_offsets, jnp.transpose(coupling, (1, 0, 2)), state, multiplier, members, static_var, courant)


def solution(mesh):
    sizes = (mesh.shape["tm"], mesh.shape["space"])
    return jax.shard_map(
        functools.partial(per_device, sizes),
        mesh=mesh,
        in_specs=(
            P("tm", None, None, "space", None),
            P("tm", None, None, "space", None),
            P("tm", None, None, None, "space", None),
            P("tm", None, None, "space", None),
            P("tm", None, None, "space", None),
            P(),
            P(),
        ),
        out_specs=P("tm", None, None, "space", None),
        check_vma=False,
    )
```

time: 148 us -> 55.3 us (0.37); the launches traced: 145 us -> 55.1 us
  other arithmetic: 66.1 us -> 0 us
  Pallas kernels: 0 us -> 53.4 us
  waiting for transfers between devices: 31.6 us -> 0 us
  starting transfers between devices: 22.3 us -> 0 us
  between operations: 11.5 us -> 0.01 us
  local copies, waits for them, and re-layouts: 10.1 us -> 1.78 us
  matrix products: 3.79 us -> 0 us
    pallas_call x0 -> x1, Pallas kernels: none -> 53.4 us  [per_device(): pl.pallas_call(functools.partial(kernel, sizes), out_shape=jax.ShapeDtype...]
    reduce_sum x1 -> x0, other arithmetic: 49.2 us -> none  [per_device(): total = jnp.sum(ensemble.astype(jnp.float32) * smoothed, axis=0)]
    ppermute x7 -> x0, waiting for transfers between devices: 31.6 us -> none  [the longest x3 22 us: padded_2(): before = lax.ppermute(last, axis, up)]
    ppermute x7 -> x0, starting transfers between devices: 22.3 us -> none  [the longest x3 18 us: padded_2(): after = lax.ppermute(leading, axis, down)]
    concatenate x1 -> x0, other arithmetic: 10.7 us -> none  [padded_2(): array = jnp.concatenate([before, array, after], axis=dim)]
    slice x7 -> x0, local copies, waits for them, and re-layouts: 5.88 us -> none  [the longest x2 4.07 us: padded_2(): last = lax.slice_in_dim(array, length - width, length, axis=dim)]
    convert_element_type x3 -> x0, other arithmetic: 5.44 us -> none  [the longest x1 5.38 us: per_device(): (ensemble.astype(jnp.float32) * lagrange[None]).astype(jnp.bfloat16)]
    dot_general x2 -> x0, matrix products: 3.79 us -> none  [tangent_step(): jnp.einsum('lvw,wlxy->vlxy', coupling, center, precision=lax.Precision.HI...]
  transfers between devices with their start and end apart: 7 -> 0, of which waited for: 4 -> 0; matrix products, arithmetic and copies ran while one was open for 3% -> 0% of each run, Pallas kernels for 0% -> 0%
where the time goes in v1:
time: 55.3 us; the launch traced here: 55.1 us
  Pallas kernels  53.4 us (97%)
  local copies, waits for them, and re-layouts  1.78 us (3%)
    pallas_call x1, Pallas kernels, per_device(): pl.pallas_call(functools.partial(kernel, sizes), out_shape=jax.ShapeDtype...  53.4 us
    unnamed x1, local copies, waits for them, and re-layouts  1.78 us

profile of v1, /device:TPU:8, one launch (start us, length us, event | category | flops | bytes accessed | tf_op | source)
XLA Modules:
  0.0 55.1 jit_solution(1836456034444307403)
XLA Ops:
  0.0 53.4 %hybrid_row.1 = f32[1,6,8,16,128]{4,3,2,1,0:T(8,128)} custom-call(s32[9]{0:T(128)} %offsets.1, f32[6,8,6]{2,1,0:T(8,128)} %bitcast.1, f32[1,6,8,16,128]{4,3,2,1,0:T(8,128)} %state_hbm.1, f32[1,6,8,16,128]{4,3,2,1,0:T(8,128)} %mult_hbm.1, bf16[1,40,6,8,16,128]{5,4,3,2,1,0:T(8,128)(2,1)} %mem_hbm.1, f32[1,6,8,16,128]{4,3,2,1,0:T(8,128)} %var_hbm.1, ...), custom_call_target="tpu_custom_call" | custom-call | tf_op jit(solution)/shard_map/hybrid_row/pallas_call | solution.py:379
  53.4 1.8 %copy.9 = f32[1,6,8,16,128]{4,3,2,1,0:T(8,128)} copy(f32[1,6,8,16,128]{4,3,2,1,0:T(8,128)} %hybrid_row.1) | data formatting | bytes 786432

commit v2 on v1

--- a/solution.py
+++ b/solution.py
@@ -65,6 +65,7 @@
     back_out,
     back_in,
     stencil,
+    relayed,
     local_sem,
     own_sem,
     mem_send,
@@ -79,6 +80,8 @@
     edge_recv,
     wind_send,
     wind_recv,
+    relay_send,
+    relay_recv,
 ):
     n_tm, n_space = sizes
     members, n_var, n_lev, width, _ = own.shape
@@ -91,9 +94,29 @@
     t_next, t_last = lax.rem(t + 1, n_tm), lax.rem(t + n_tm - 1, n_tm)
     s_next, s_last = lax.rem(s + 1, n_space), lax.rem(s + n_space - 1, n_space)
 
+    planes = n_space // 4
+    run = (s // (2 * planes)) * (2 * planes)
+    z = lax.rem(s // 2, planes)
+    outer = (z == 0) | (z == planes - 1)
+    relay_of = jnp.where(z == 0, run + 3, run + 2 * (planes - 2))
+    is_relay = (s == run + 3) | (s == run + 2 * (planes - 2))
+    served = jnp.where(z == 1, run, run + 2 * (planes - 1))
+
     barrier = pltpu.get_barrier_semaphore()
-    for peer in ((t, s_next), (t, s_last), (t_last, s), (t_last, s_next), (t_last, s_last)):
+
+    def greet(*peer):
         pl.semaphore_signal(barrier, inc=1, device_id=peer, device_id_type=MESH)
+
+    greet(t, s_next)
+    greet(t, s_last)
+    greet(t_last, s_next)
+    greet(t_last, s_last)
+    greet(jnp.where(outer, t, t_last), jnp.where(outer, relay_of, s))
+
+    @pl.when(is_relay)
+    def _():
+        greet(t_last, served)
+        greet(t_last, served + 1)
 
     load_state = pltpu.make_async_copy(state_hbm.at[0], state, local_sem.at[0])
     load_wind = pltpu.make_async_copy(
@@ -181,12 +204,29 @@
             (t, neighbour(1 - h)),
         )
 
-    pl.semaphore_wait(barrier, 5)
+    pl.semaphore_wait(barrier, jnp.where(is_relay, 7, 5))
     for h in range(2):
         lam_copy(h).start()
     for h in range(2):
         mem_copy(h, 0).start()
-    state_copy.start()
+
+    @pl.when(~outer)
+    def _():
+        state_copy.start()
+
+    def relay_in(c, where):
+        return send(
+            state_hbm.at[0], relayed.at[c], relay_send.at[c], relay_recv.at[c], (t_next, where)
+        )
+
+    def relay_out(c):
+        return send(
+            relayed.at[c],
+            prev.at[:, :, pl.ds(8, width)],
+            relay_send.at[2 + c],
+            state_recv.at[0],
+            (t, served + c),
+        )
 
     def start_members(k, carry):
         for h in range(2):
@@ -194,6 +234,12 @@
         return carry
 
     lax.fori_loop(1, chunks // 2, start_members, 0)
+
+    @pl.when(outer)
+    def _():
+        relay_in(parity, relay_of).start()
+
+    lax.fori_loop(chunks // 2, chunks, start_members, 0)
 
     def start_own(v, carry):
         d2d_side = 1 - parity
@@ -228,7 +274,6 @@
     for h in range(2):
         edge_copy(h).start()
         wind_copy(h).start()
-    lax.fori_loop(chunks // 2, chunks, start_members, 0)
     load_lam.wait()
 
     def one_level(side, v, level):
@@ -279,6 +324,14 @@
 
         lax.fori_loop(0, LEVELS_PER_CHUNK, each, 0)
         back_copy(side, k).start()
+
+        for c, at in ((0, chunks // 2), (1, (3 * chunks) // 4)):
+
+            @pl.when(is_relay & (j == 2 * at))
+            def _():
+                relay_in(c, s).wait_recv()
+                relay_out(c).start()
+
         return carry
 
     def lam_copy_wait(h):
@@ -290,8 +343,7 @@
             (t, neighbour(1 - h)),
         ).wait_recv()
 
-    middle = 2 * ((3 * chunks) // 4)
-    lax.fori_loop(0, middle, step, 0)
+    lax.fori_loop(0, 2 * chunks, step, 0)
 
     state_copy.wait_recv()
     for h in range(2):
@@ -338,7 +390,6 @@
         return carry
 
     lax.fori_loop(0, n_lev, tangent, 0)
-    lax.fori_loop(middle, 2 * chunks, step, 0)
 
     def drain(k, carry):
         for h in range(2):
@@ -360,7 +411,19 @@
             out[0, full_v, :, keep_lo:keep_hi] = (
                 base[full_v, :, keep_lo:keep_hi] + scale * total[full_v, :, keep_lo:keep_hi]
             )
-    state_copy.wait_send()
+    @pl.when(~outer)
+    def _():
+        state_copy.wait_send()
+
+    @pl.when(outer)
+    def _():
+        relay_in(parity, relay_of).wait_send()
+
+    @pl.when(is_relay)
+    def _():
+        for c in range(2):
+            relay_out(c).wait_send()
+
     for h in range(2):
         lam_copy(h).wait_send()
         edge_copy(h).wait_send()
@@ -374,7 +437,7 @@
     size = GROUP * (width + RADIUS)
     f32, bf16 = jnp.float32, jnp.bfloat16
     dma = pltpu.SemaphoreType.DMA
-    hbm = pl.BlockSpec(memory_space=pl.ANY)
+    hbm = pl.BlockSpec(memory_space=pltpu.HBM)
     smem = pl.BlockSpec(memory_space=pltpu.SMEM)
     return pl.pallas_call(
         functools.partial(kernel, sizes),
@@ -399,6 +462,7 @@
             pltpu.VMEM((2, half, n_lev, RADIUS, lanes), f32),
             pltpu.VMEM((2, half, n_lev, RADIUS, lanes), f32),
             pltpu.VMEM((2, 2, size, size), bf16),
+            pltpu.VMEM((2, n_var, n_lev, width, lanes), f32),
             dma((4,)),
             dma((n_var,)),
             dma((2, chunks)),
@@ -413,12 +477,14 @@
             dma((2,)),
             dma((2,)),
             dma((2,)),
+            dma((4,)),
+            dma((2,)),
         ],
         compiler_params=pltpu.CompilerParams(
-            collective_id=0, has_side_effects=True, vmem_limit_bytes=67043328
+            collective_id=0, has_side_effects=True, vmem_limit_bytes=48 * 1024 * 1024
         ),
         name="hybrid_row",
-    )(loc_offsets, jnp.transpose(coupling, (1, 0, 2)), state, multiplier, members, static_var, courant)
+    )(*[pltpu.with_memory_space_constraint(x, pltpu.HBM) for x in (loc_offsets, jnp.transpose(coupling, (1, 0, 2)), state, multiplier, members, static_var, courant)])
 
 
 def solution(mesh):

time: 55.3 us -> 43.5 us (0.79); the launches traced: 55.1 us -> 42.7 us
  Pallas kernels: 53.4 us -> 42 us
  local copies, waits for them, and re-layouts: 1.78 us -> 0.75 us
    pallas_call x1, Pallas kernels: 53.4 us -> 42 us  [per_device(): pl.pallas_call(functools.partial(kernel, sizes), out_shape=jax.ShapeDtype...]
    unnamed x1, local copies, waits for them, and re-layouts: 1.78 us -> 0.75 us
where the time goes in v2:
time: 43.5 us; the launch traced here: 42.7 us
  Pallas kernels  42 us (97%)
  local copies, waits for them, and re-layouts  0.75 us (2%)
    pallas_call x1, Pallas kernels, per_device(): pl.pallas_call(functools.partial(kernel, sizes), out_shape=jax.ShapeDtype...  42 us

profile of v2, /device:TPU:8, one launch (start us, length us, event | category | flops | bytes accessed | tf_op | source)
XLA Modules:
  0.0 42.7 jit_solution(12424923837562364062)
XLA Ops:
  0.0 42.0 %hybrid_row.1 = f32[1,6,8,16,128]{4,3,2,1,0:T(8,128)S(1)} custom-call(s32[9]{0:T(128)} %offsets.1, f32[6,8,6]{2,1,0:T(8,128)} %bitcast.1, f32[1,6,8,16,128]{4,3,2,1,0:T(8,128)} %state_hbm.1, f32[1,6,8,16,128]{4,3,2,1,0:T(8,128)} %mult_hbm.1, bf16[1,40,6,8,16,128]{5,4,3,2,1,0:T(8,128)(2,1)} %mem_hbm.1, f32[1,6,8,16,128]{4,3,2,1,0:T(8,128)} %var_hbm.1, ...), custom_call_target="tpu_custom_call" | custom-call | tf_op jit(solution)/shard_map/hybrid_row/pallas_call | solution.py:442
  42.0 0.7 %copy.9 = f32[1,6,8,16,128]{4,3,2,1,0:T(8,128)} copy(f32[1,6,8,16,128]{4,3,2,1,0:T(8,128)S(1)} %hybrid_row.1) | data formatting | bytes 786432

commit v3 on v2

--- a/solution.py
+++ b/solution.py
@@ -8,6 +8,8 @@
 
 MESH = pl.DeviceIdType.MESH
 GROUP = 10
+DEPTH = 256
+LEAD = 4
 RADIUS = 8
 LEVELS_PER_CHUNK = 2
 
@@ -23,8 +25,7 @@
 
 
 def stencil_matrix(offsets, side, width, rows, row_start):
-    size = GROUP * (width + RADIUS)
-    shape = (rows, size)
+    shape = (rows, DEPTH)
     row = lax.broadcasted_iota(jnp.int32, shape, 0) + row_start
     col = lax.broadcasted_iota(jnp.int32, shape, 1)
     row_member, row_column, row_halo = column_of(row, width, side)
@@ -40,8 +41,8 @@
 
 def kernel(
     sizes,
-    offsets,
-    coupling,
+    offsets_hbm,
+    coupling_hbm,
     state_hbm,
     mult_hbm,
     mem_hbm,
@@ -66,6 +67,10 @@
     back_in,
     stencil,
     relayed,
+    extra,
+    extra_lam,
+    offsets,
+    coupling,
     local_sem,
     own_sem,
     mem_send,
@@ -82,10 +87,12 @@
     wind_recv,
     relay_send,
     relay_recv,
+    extra_send,
+    extra_recv,
 ):
     n_tm, n_space = sizes
     members, n_var, n_lev, width, _ = own.shape
-    half = n_var // 2
+    half, half_lev = n_var // 2, n_lev // 2
     per_var = n_lev // LEVELS_PER_CHUNK
     chunks = half * per_var
     t = lax.axis_index("tm")
@@ -99,8 +106,11 @@
     z = lax.rem(s // 2, planes)
     outer = (z == 0) | (z == planes - 1)
     relay_of = jnp.where(z == 0, run + 3, run + 2 * (planes - 2))
+    wrap = ((z == 0) & (parity == 0)) | ((z == planes - 1) & (parity == 1))
+    late = outer & ~wrap
     is_relay = (s == run + 3) | (s == run + 2 * (planes - 2))
-    served = jnp.where(z == 1, run, run + 2 * (planes - 1))
+    served = jnp.where(z == 1, run, run + 2 * planes - 1)
+    served_late = jnp.where(z == 1, run + 1, run + 2 * planes - 2)
 
     barrier = pltpu.get_barrier_semaphore()
 
@@ -111,12 +121,16 @@
     greet(t, s_last)
     greet(t_last, s_next)
     greet(t_last, s_last)
-    greet(jnp.where(outer, t, t_last), jnp.where(outer, relay_of, s))
+    greet(jnp.where(wrap, t, t_last), jnp.where(wrap, relay_of, s))
+
+    @pl.when(late)
+    def _():
+        greet(t, relay_of)
 
     @pl.when(is_relay)
     def _():
         greet(t_last, served)
-        greet(t_last, served + 1)
+        greet(t_last, served_late)
 
     load_state = pltpu.make_async_copy(state_hbm.at[0], state, local_sem.at[0])
     load_wind = pltpu.make_async_copy(
@@ -124,13 +138,21 @@
     )
     load_lam = pltpu.make_async_copy(mult_hbm.at[0], lam, local_sem.at[2])
     load_var = pltpu.make_async_copy(var_hbm.at[0], var, local_sem.at[3])
-    load_state.start()
-    load_wind.start()
-    load_lam.start()
-    load_var.start()
-
     def load_own(v):
         return pltpu.make_async_copy(mem_hbm.at[0, :, v], own.at[:, v], own_sem.at[v])
+
+    load_offsets = pltpu.make_async_copy(offsets_hbm, offsets, local_sem.at[4])
+    load_coupling = pltpu.make_async_copy(coupling_hbm, coupling, local_sem.at[5])
+    load_lam.start()
+    for v in range(half):
+        load_own(v).start()
+        load_own(half + v).start()
+        if v == 0:
+            load_state.start()
+            load_wind.start()
+    load_offsets.start()
+    load_coupling.start()
+    load_var.start()
 
     def neighbour(side):
         return lax.rem(s + n_space - 1 + 2 * side, n_space)
@@ -150,7 +172,7 @@
         levels = pl.ds(level, LEVELS_PER_CHUNK)
         rows = pl.ds(pl.multiple_of((1 - h) * RADIUS, RADIUS), RADIUS)
         return send(
-            mem_hbm.at[0, :, half * h + v, levels, rows],
+            own.at[:, half * h + v, levels, rows],
             halo.at[h, :, v, levels],
             mem_send.at[h, k],
             mem_recv.at[h, k],
@@ -160,7 +182,7 @@
     def lam_copy(h):
         rows = pl.ds((1 - h) * RADIUS, RADIUS)
         return send(
-            mult_hbm.at[0, pl.ds(half * h, half), :, rows],
+            lam.at[pl.ds(half * h, half), :, rows],
             lam_halo.at[h],
             lam_send.at[h],
             lam_recv.at[h],
@@ -178,12 +200,52 @@
             (t, neighbour(h)),
         )
 
-    state_copy = send(
-        state_hbm.at[0],
-        prev.at[:, :, pl.ds(8, width)],
-        state_send.at[0],
-        state_recv.at[0],
-        (t_next, s),
+    def part_of(ref, p):
+        return ref.at[:, pl.ds(half_lev * p, half_lev)]
+
+    def state_copy(p):
+        return send(
+            part_of(state_hbm.at[0], p),
+            part_of(prev, p).at[:, :, pl.ds(8, width)],
+            state_send.at[p],
+            state_recv.at[p],
+            (t_next, s),
+        )
+
+    def relay_in(slot):
+        return send(
+            part_of(state_hbm.at[0], min(slot, 1)),
+            relayed.at[slot],
+            relay_send.at[slot],
+            relay_recv.at[slot],
+            (t_next, relay_of),
+        )
+
+    def relay_out(slot):
+        return send(
+            relayed.at[slot],
+            part_of(prev, min(slot, 1)).at[:, :, pl.ds(8, width)],
+            relay_send.at[3 + slot],
+            state_recv.at[min(slot, 1)],
+            (t, served if slot < 2 else served_late),
+        )
+
+    last = chunks - 1
+    last_levels = pl.ds(n_lev - LEVELS_PER_CHUNK, LEVELS_PER_CHUNK)
+    facing = pl.ds(pl.multiple_of(parity * RADIUS, RADIUS), RADIUS)
+    extra_copy = send(
+        own.at[:, half * parity + half - 1, last_levels, facing],
+        extra,
+        extra_send.at[0],
+        extra_recv.at[0],
+        (t, neighbour(parity)),
+    )
+    extra_lam_copy = send(
+        lam.at[half * parity + half - 1, last_levels, facing],
+        extra_lam,
+        extra_send.at[1],
+        extra_recv.at[1],
+        (t, neighbour(parity)),
     )
 
     def edge_copy(h):
@@ -204,49 +266,36 @@
             (t, neighbour(1 - h)),
         )
 
-    pl.semaphore_wait(barrier, jnp.where(is_relay, 7, 5))
+    pl.semaphore_wait(barrier, jnp.where(is_relay, 7, jnp.where(late, 6, 5)))
+    load_lam.wait()
     for h in range(2):
         lam_copy(h).start()
+    load_own(0).wait()
+    load_own(half).wait()
     for h in range(2):
         mem_copy(h, 0).start()
 
     @pl.when(~outer)
     def _():
-        state_copy.start()
-
-    def relay_in(c, where):
-        return send(
-            state_hbm.at[0], relayed.at[c], relay_send.at[c], relay_recv.at[c], (t_next, where)
-        )
-
-    def relay_out(c):
-        return send(
-            relayed.at[c],
-            prev.at[:, :, pl.ds(8, width)],
-            relay_send.at[2 + c],
-            state_recv.at[0],
-            (t, served + c),
-        )
+        state_copy(0).start()
+        state_copy(1).start()
 
     def start_members(k, carry):
         for h in range(2):
             mem_copy(h, k).start()
         return carry
 
-    lax.fori_loop(1, chunks // 2, start_members, 0)
-
-    @pl.when(outer)
-    def _():
-        relay_in(parity, relay_of).start()
-
-    lax.fori_loop(chunks // 2, chunks, start_members, 0)
-
-    def start_own(v, carry):
-        d2d_side = 1 - parity
-        load_own(lax.rem(v // 2 + half * lax.rem(d2d_side + lax.rem(v, 2), 2), n_var)).start()
-        return carry
-
-    lax.fori_loop(0, n_var, start_own, 0)
+    @pl.when(wrap)
+    def _():
+        relay_in(0).start()
+        relay_in(1).start()
+        extra_lam_copy.start()
+
+    lax.fori_loop(1, per_var, start_members, 0)
+
+    @pl.when(late)
+    def _():
+        relay_in(2).start()
 
     load_state.wait()
     load_wind.wait()
@@ -256,6 +305,18 @@
     wind_edge[0] = wind[:, :, 8 + width - 1]
     wind_edge[1] = wind[:, :, 8]
 
+    for h in range(2):
+        edge_copy(h).start()
+        wind_copy(h).start()
+    for v in range(1, half):
+        load_own(v).wait()
+        load_own(half + v).wait()
+        lax.fori_loop(per_var * v, per_var * (v + 1), start_members, 0)
+
+    @pl.when(wrap)
+    def _():
+        extra_copy.start()
+
     size = GROUP * (width + RADIUS)
     block = 48
 
@@ -264,53 +325,75 @@
         row_start = pl.multiple_of(lax.rem(step, size // block) * block, block)
         matrix = stencil_matrix(offsets, side, width, block, row_start)
         high = matrix.astype(jnp.bfloat16)
-        stencil[side, 0, pl.ds(row_start, block)] = high
-        stencil[side, 1, pl.ds(row_start, block)] = (matrix - high.astype(jnp.float32)).astype(
-            jnp.bfloat16
-        )
-        return carry
-
+        rows = pl.ds(row_start, block)
+        stencil[side, rows, :DEPTH] = high
+        stencil[side, rows, DEPTH:] = (matrix - high.astype(jnp.float32)).astype(jnp.bfloat16)
+        return carry
+
+    load_offsets.wait()
     lax.fori_loop(0, 2 * (size // block), build, 0)
-    for h in range(2):
-        edge_copy(h).start()
-        wind_copy(h).start()
-    load_lam.wait()
-
-    def one_level(side, v, level):
-        full_v = half * side + v
+    def sums(side, full_v, level, lam_far, far_fields, near_products):
         lam_own = lam[full_v, level]
-        lam_far = lam_halo[side, v, level]
         own_sum = jnp.zeros((width, 128), jnp.float32)
         far_sum = jnp.zeros((RADIUS, 128), jnp.float32)
         for pair in range(members // (2 * GROUP)):
             fields, products = [], []
             for q in (2 * pair, 2 * pair + 1):
                 near = own[pl.ds(q * GROUP, GROUP), full_v, level].astype(jnp.float32)
-                far = halo[side, pl.ds(q * GROUP, GROUP), v, level].astype(jnp.float32)
+                far = far_fields(pl.ds(q * GROUP, GROUP)).astype(jnp.float32)
                 fields.append((near, far))
-                near = (near * lam_own[None]).reshape(GROUP * width, 128)
+                near = near * lam_own[None] if near_products else jnp.zeros_like(near)
+                near = near.reshape(GROUP * width, 128)
                 far = (far * lam_far[None]).reshape(GROUP * RADIUS, 128)
-                products.append(jnp.concatenate([near, far], axis=0).astype(jnp.bfloat16))
+                rest = jnp.zeros((DEPTH - GROUP * (width + RADIUS), 128), jnp.float32)
+                product = jnp.concatenate([near, far, rest], axis=0).astype(jnp.bfloat16)
+                products.append(jnp.concatenate([product, product], axis=0))
             rhs = jnp.concatenate(products, axis=1)
-            smooth = jnp.dot(stencil[side, 0], rhs, preferred_element_type=jnp.float32)
-            smooth = smooth + jnp.dot(stencil[side, 1], rhs, preferred_element_type=jnp.float32)
+            smooth = jnp.dot(stencil[side], rhs, preferred_element_type=jnp.float32)
             for i, (near, far) in enumerate(fields):
                 part = smooth[:, 128 * i : 128 * (i + 1)]
                 own_part = part[: GROUP * width].reshape(GROUP, width, 128)
                 far_part = part[GROUP * width :].reshape(GROUP, RADIUS, 128)
                 own_sum = own_sum + jnp.sum(near * own_part, axis=0)
                 far_sum = far_sum + jnp.sum(far * far_part, axis=0)
-        total[full_v, level] = own_sum
-        back_out[side, v, level] = far_sum
+        return own_sum, far_sum
+
+    def one_level(side, v, level):
+        total[half * side + v, level], back_out[side, v, level] = sums(
+            side,
+            half * side + v,
+            level,
+            lam_halo[side, v, level],
+            lambda group: halo[side, group, v, level],
+            True,
+        )
+
+    def extra_level(d, carry):
+        level = n_lev - LEVELS_PER_CHUNK + d
+        own_sum, _ = sums(
+            parity,
+            half * (1 - parity) + half - 1,
+            level,
+            extra_lam[d],
+            lambda group: extra[group, d],
+            False,
+        )
+        back_in[1 - parity, half - 1, level] = jnp.where(
+            parity == 0, own_sum[:RADIUS], own_sum[width - RADIUS :]
+        )
+        return carry
 
     def step(j, carry):
-        k, over_ici = j // 2, lax.rem(j, 2)
+        turn = j - LEAD
+        in_turn = (turn >= 0) & (j < 2 * chunks - LEAD)
+        over_ici = jnp.where(in_turn, 1 - lax.rem(turn + 2 * chunks, 2), jnp.where(turn < 0, 0, 1))
+        k = jnp.where(
+            in_turn,
+            jnp.where(over_ici == 1, turn // 2, LEAD + turn // 2),
+            jnp.where(turn < 0, j, j - chunks),
+        )
         side = lax.rem(parity + 1 - over_ici, 2)
         v, level = k // per_var, lax.rem(k, per_var) * LEVELS_PER_CHUNK
-
-        @pl.when(lax.rem(k, per_var) == 0)
-        def _():
-            load_own(half * side + v).wait()
 
         @pl.when(k == 0)
         def _():
@@ -322,21 +405,28 @@
             one_level(side, v, level + d)
             return c
 
-        lax.fori_loop(0, LEVELS_PER_CHUNK, each, 0)
-        back_copy(side, k).start()
-
-        for c, at in ((0, chunks // 2), (1, (3 * chunks) // 4)):
-
-            @pl.when(is_relay & (j == 2 * at))
+        lax.fori_loop(0, LEVELS_PER_CHUNK, each, 0, unroll=True)
+
+        @pl.when(~(wrap & (side == parity) & (k == last)))
+        def _():
+            back_copy(side, k).start()
+
+        for slot, at in ((0, chunks // 3), (1, chunks // 2), (2, (2 * chunks) // 3)):
+
+            @pl.when(is_relay & (over_ici == 1) & (k == at))
             def _():
-                relay_in(c, s).wait_recv()
-                relay_out(c).start()
+                relay_in(slot).wait_recv()
+                relay_out(slot).start()
+
+        @pl.when(late & (over_ici == 1) & (k == (2 * chunks) // 3))
+        def _():
+            state_copy(0).start()
 
         return carry
 
     def lam_copy_wait(h):
         send(
-            mult_hbm.at[0, pl.ds(0, half), :, pl.ds(0, RADIUS)],
+            lam.at[pl.ds(0, half), :, pl.ds(0, RADIUS)],
             lam_halo.at[h],
             lam_send.at[h],
             lam_recv.at[h],
@@ -345,7 +435,61 @@
 
     lax.fori_loop(0, 2 * chunks, step, 0)
 
-    state_copy.wait_recv()
+    def drain_sends(k, carry):
+        for h in range(2):
+            mem_copy(h, k).wait_send()
+        return carry
+
+    def drain_back(k, carry):
+        for h in range(2):
+
+            @pl.when(~(wrap & (h == 1 - parity) & (k == last)))
+            def _():
+                back_copy(h, k).wait_recv()
+
+        return carry
+
+    def drain_back_sends(k, carry):
+        for h in range(2):
+
+            @pl.when(~(wrap & (h == parity) & (k == last)))
+            def _():
+                back_copy(h, k).wait_send()
+
+        return carry
+
+    lax.fori_loop(0, chunks, drain_sends, 0)
+    load_coupling.wait()
+
+    @pl.when(~wrap)
+    def _():
+        state_copy(0).wait_send()
+
+    @pl.when(~outer)
+    def _():
+        state_copy(1).wait_send()
+
+    @pl.when(wrap)
+    def _():
+        relay_in(0).wait_send()
+        relay_in(1).wait_send()
+        extra_copy.wait_send()
+        extra_lam_copy.wait_send()
+
+    @pl.when(late)
+    def _():
+        relay_in(2).wait_send()
+
+    @pl.when(is_relay)
+    def _():
+        for slot in range(3):
+            relay_out(slot).wait_send()
+
+    for h in range(2):
+        lam_copy(h).wait_send()
+        edge_copy(h).wait_send()
+        wind_copy(h).wait_send()
+
     for h in range(2):
         edge_copy(h).wait_recv()
         wind_copy(h).wait_recv()
@@ -353,9 +497,6 @@
     padded = width + 16
     rows = lax.broadcasted_iota(jnp.int32, (padded, 128), 0)
     lanes = lax.broadcasted_iota(jnp.int32, (padded, 128), 1)
-    for c in range(2):
-        prev[:, :, 6 + c] = state_halo[0, c]
-        prev[:, :, 8 + width + c] = state_halo[1, c]
     wind[:, :, 7] = wind_halo[0]
     wind[:, :, 8 + width] = wind_halo[1]
     first = jnp.where(t == 0, 0.0, 1.0)
@@ -389,45 +530,34 @@
             )
         return carry
 
-    lax.fori_loop(0, n_lev, tangent, 0)
-
-    def drain(k, carry):
-        for h in range(2):
-            back_copy(h, k).wait_recv()
-            back_copy(h, k).wait_send()
-            mem_copy(h, k).wait_send()
-        return carry
-
-    lax.fori_loop(0, chunks, drain, 0)
+    for p in (1, 0):
+        state_copy(p).wait_recv()
+        levels = pl.ds(half_lev * p, half_lev)
+        for c in range(2):
+            prev[:, levels, 6 + c] = state_halo[0, c, :, levels]
+            prev[:, levels, 8 + width + c] = state_halo[1, c, :, levels]
+        lax.fori_loop(half_lev * p, half_lev * (p + 1), tangent, 0)
+
+    @pl.when(wrap)
+    def _():
+        extra_copy.wait_recv()
+        extra_lam_copy.wait_recv()
+        lax.fori_loop(0, LEVELS_PER_CHUNK, extra_level, 0)
+
+
     scale = 0.5 / (members - 1)
+
+    def compose(v, carry):
+        out[0, v] = base[v] + scale * total[v]
+        return carry
+
+    lax.fori_loop(0, n_var, compose, 0)
+    lax.fori_loop(0, chunks, drain_back_sends, 0)
+    lax.fori_loop(0, chunks, drain_back, 0)
     for h in range(2):
+        edge = pl.ds(0, RADIUS) if h == 1 else pl.ds(width - RADIUS, RADIUS)
         for v in range(half):
-            full_v = half * h + v
-            lo, hi = (0, RADIUS) if h == 1 else (width - RADIUS, width)
-            keep_lo, keep_hi = (RADIUS, width) if h == 1 else (0, width - RADIUS)
-            out[0, full_v, :, lo:hi] = base[full_v, :, lo:hi] + scale * (
-                total[full_v, :, lo:hi] + back_in[h, v]
-            )
-            out[0, full_v, :, keep_lo:keep_hi] = (
-                base[full_v, :, keep_lo:keep_hi] + scale * total[full_v, :, keep_lo:keep_hi]
-            )
-    @pl.when(~outer)
-    def _():
-        state_copy.wait_send()
-
-    @pl.when(outer)
-    def _():
-        relay_in(parity, relay_of).wait_send()
-
-    @pl.when(is_relay)
-    def _():
-        for c in range(2):
-            relay_out(c).wait_send()
-
-    for h in range(2):
-        lam_copy(h).wait_send()
-        edge_copy(h).wait_send()
-        wind_copy(h).wait_send()
+            out[0, half * h + v, :, edge] += scale * back_in[h, v]
 
 
 def per_device(sizes, state, multiplier, members, static_var, courant, coupling, loc_offsets):
@@ -438,11 +568,12 @@
     f32, bf16 = jnp.float32, jnp.bfloat16
     dma = pltpu.SemaphoreType.DMA
     hbm = pl.BlockSpec(memory_space=pltpu.HBM)
-    smem = pl.BlockSpec(memory_space=pltpu.SMEM)
+    offsets_shape = loc_offsets.shape
+    coupling_shape = (n_var, n_lev, n_var)
     return pl.pallas_call(
         functools.partial(kernel, sizes),
         out_shape=jax.ShapeDtypeStruct(state.shape, f32),
-        in_specs=[smem, smem, hbm, hbm, hbm, hbm, hbm],
+        in_specs=[hbm] * 7,
         out_specs=pl.BlockSpec(memory_space=pltpu.VMEM),
         scratch_shapes=[
             pltpu.VMEM((n_mem, n_var, n_lev, width, lanes), bf16),
@@ -461,9 +592,13 @@
             pltpu.VMEM((n_var, n_lev, width, lanes), f32),
             pltpu.VMEM((2, half, n_lev, RADIUS, lanes), f32),
             pltpu.VMEM((2, half, n_lev, RADIUS, lanes), f32),
-            pltpu.VMEM((2, 2, size, size), bf16),
-            pltpu.VMEM((2, n_var, n_lev, width, lanes), f32),
-            dma((4,)),
+            pltpu.VMEM((2, size, 2 * DEPTH), bf16),
+            pltpu.VMEM((3, n_var, n_lev // 2, width, lanes), f32),
+            pltpu.VMEM((n_mem, LEVELS_PER_CHUNK, RADIUS, lanes), bf16),
+            pltpu.VMEM((LEVELS_PER_CHUNK, RADIUS, lanes), f32),
+            pltpu.SMEM(offsets_shape, jnp.int32),
+            pltpu.SMEM(coupling_shape, f32),
+            dma((6,)),
             dma((n_var,)),
             dma((2, chunks)),
             dma((2, chunks)),
@@ -471,13 +606,15 @@
             dma((2, chunks)),
             dma((2,)),
             dma((2,)),
-            dma((1,)),
-            dma((1,)),
-            dma((2,)),
-            dma((2,)),
-            dma((2,)),
-            dma((2,)),
-            dma((4,)),
+            dma((2,)),
+            dma((2,)),
+            dma((2,)),
+            dma((2,)),
+            dma((2,)),
+            dma((2,)),
+            dma((6,)),
+            dma((3,)),
+            dma((2,)),
             dma((2,)),
         ],
         compiler_params=pltpu.CompilerParams(

time: 43.5 us -> 41.9 us (0.963); the launches traced: 42.7 us -> 41.9 us
  Pallas kernels: 42 us -> 41.1 us
    pallas_call x1, Pallas kernels: 42 us -> 41.1 us  [per_device(): pl.pallas_call(functools.partial(kernel, sizes), out_shape=jax.ShapeDtype...]
where the time goes in v3:
time: 41.9 us
  Pallas kernels  41.1 us (98%)
  local copies, waits for them, and re-layouts  0.75 us (2%)
    pallas_call x1, Pallas kernels, per_device(): pl.pallas_call(functools.partial(kernel, sizes), out_shape=jax.ShapeDtype...  41.1 us

profile of v3, /device:TPU:8, one launch (start us, length us, event | category | flops | bytes accessed | tf_op | source)
XLA Modules:
  0.0 41.9 jit_solution(17323888989720904895)
XLA Ops:
  0.0 41.1 %hybrid_row.1 = f32[1,6,8,16,128]{4,3,2,1,0:T(8,128)S(1)} custom-call(s32[9]{0:T(128)} %offsets_hbm.1, f32[6,8,6]{2,1,0:T(8,128)} %bitcast.1, f32[1,6,8,16,128]{4,3,2,1,0:T(8,128)} %state_hbm.1, f32[1,6,8,16,128]{4,3,2,1,0:T(8,128)} %mult_hbm.1, bf16[1,40,6,8,16,128]{5,4,3,2,1,0:T(8,128)(2,1)} %mem_hbm.1, f32[1,6,8,16,128]{4,3,2,1,0:T(8,128)} %var_hbm.1, ...), custom_call_target="tpu_custom_call" | custom-call | tf_op jit(solution)/shard_map/hybrid_row/pallas_call | solution.py:573
  41.1 0.7 %copy.9 = f32[1,6,8,16,128]{4,3,2,1,0:T(8,128)} copy(f32[1,6,8,16,128]{4,3,2,1,0:T(8,128)S(1)} %hybrid_row.1) | data formatting | bytes 786432

commit v4 on v3

--- a/solution.py
+++ b/solution.py
@@ -66,6 +66,8 @@
     back_out,
     back_in,
     stencil,
+    lam_edge,
+    extra_lam_edge,
     relayed,
     extra,
     extra_lam,
@@ -180,9 +182,8 @@
         )
 
     def lam_copy(h):
-        rows = pl.ds((1 - h) * RADIUS, RADIUS)
-        return send(
-            lam.at[pl.ds(half * h, half), :, rows],
+        return send(
+            lam_edge.at[h],
             lam_halo.at[h],
             lam_send.at[h],
             lam_recv.at[h],
@@ -241,7 +242,7 @@
         (t, neighbour(parity)),
     )
     extra_lam_copy = send(
-        lam.at[half * parity + half - 1, last_levels, facing],
+        extra_lam_edge,
         extra_lam,
         extra_send.at[1],
         extra_recv.at[1],
@@ -269,11 +270,14 @@
     pl.semaphore_wait(barrier, jnp.where(is_relay, 7, jnp.where(late, 6, 5)))
     load_lam.wait()
     for h in range(2):
-        lam_copy(h).start()
+        edge = lam[half * h : half * (h + 1), :, (1 - h) * RADIUS : (2 - h) * RADIUS]
+        lam_edge[h] = edge.astype(jnp.bfloat16)
+    extra_lam_edge[...] = lam[half * parity + half - 1, last_levels, facing].astype(jnp.bfloat16)
     load_own(0).wait()
     load_own(half).wait()
     for h in range(2):
         mem_copy(h, 0).start()
+        lam_copy(h).start()
 
     @pl.when(~outer)
     def _():
@@ -359,14 +363,16 @@
         return own_sum, far_sum
 
     def one_level(side, v, level):
-        total[half * side + v, level], back_out[side, v, level] = sums(
+        own_sum, far_sum = sums(
             side,
             half * side + v,
             level,
-            lam_halo[side, v, level],
+            lam_halo[side, v, level].astype(jnp.float32),
             lambda group: halo[side, group, v, level],
             True,
         )
+        total[half * side + v, level] = own_sum
+        back_out[side, v, level] = far_sum.astype(jnp.bfloat16)
 
     def extra_level(d, carry):
         level = n_lev - LEVELS_PER_CHUNK + d
@@ -374,13 +380,13 @@
             parity,
             half * (1 - parity) + half - 1,
             level,
-            extra_lam[d],
+            extra_lam[d].astype(jnp.float32),
             lambda group: extra[group, d],
             False,
         )
-        back_in[1 - parity, half - 1, level] = jnp.where(
-            parity == 0, own_sum[:RADIUS], own_sum[width - RADIUS :]
-        )
+        near = jnp.where(parity == 0, own_sum[:RADIUS], own_sum[width - RADIUS :])
+        total[half * (1 - parity) + half - 1, level, facing] += near
+        back_in[1 - parity, half - 1, level] = jnp.zeros((RADIUS, 128), jnp.bfloat16)
         return carry
 
     def step(j, carry):
@@ -426,7 +432,7 @@
 
     def lam_copy_wait(h):
         send(
-            lam.at[pl.ds(0, half), :, pl.ds(0, RADIUS)],
+            lam_edge.at[h],
             lam_halo.at[h],
             lam_send.at[h],
             lam_recv.at[h],
@@ -557,7 +563,7 @@
     for h in range(2):
         edge = pl.ds(0, RADIUS) if h == 1 else pl.ds(width - RADIUS, RADIUS)
         for v in range(half):
-            out[0, half * h + v, :, edge] += scale * back_in[h, v]
+            out[0, half * h + v, :, edge] += scale * back_in[h, v].astype(jnp.float32)
 
 
 def per_device(sizes, state, multiplier, members, static_var, courant, coupling, loc_offsets):
@@ -579,7 +585,7 @@
             pltpu.VMEM((n_mem, n_var, n_lev, width, lanes), bf16),
             pltpu.VMEM((2, n_mem, half, n_lev, RADIUS, lanes), bf16),
             pltpu.VMEM((n_var, n_lev, width, lanes), f32),
-            pltpu.VMEM((2, half, n_lev, RADIUS, lanes), f32),
+            pltpu.VMEM((2, half, n_lev, RADIUS, lanes), bf16),
             pltpu.VMEM((n_var, n_lev, width, lanes), f32),
             pltpu.VMEM((n_var, n_lev, width + 16, lanes), f32),
             pltpu.VMEM((n_var, n_lev, width, lanes), f32),
@@ -590,12 +596,14 @@
             pltpu.VMEM((2, 2, n_lev, lanes), f32),
             pltpu.VMEM((n_var, n_lev, width, lanes), f32),
             pltpu.VMEM((n_var, n_lev, width, lanes), f32),
-            pltpu.VMEM((2, half, n_lev, RADIUS, lanes), f32),
-            pltpu.VMEM((2, half, n_lev, RADIUS, lanes), f32),
+            pltpu.VMEM((2, half, n_lev, RADIUS, lanes), bf16),
+            pltpu.VMEM((2, half, n_lev, RADIUS, lanes), bf16),
             pltpu.VMEM((2, size, 2 * DEPTH), bf16),
+            pltpu.VMEM((2, half, n_lev, RADIUS, lanes), bf16),
+            pltpu.VMEM((LEVELS_PER_CHUNK, RADIUS, lanes), bf16),
             pltpu.VMEM((3, n_var, n_lev // 2, width, lanes), f32),
             pltpu.VMEM((n_mem, LEVELS_PER_CHUNK, RADIUS, lanes), bf16),
-            pltpu.VMEM((LEVELS_PER_CHUNK, RADIUS, lanes), f32),
+            pltpu.VMEM((LEVELS_PER_CHUNK, RADIUS, lanes), bf16),
             pltpu.SMEM(offsets_shape, jnp.int32),
             pltpu.SMEM(coupling_shape, f32),
             dma((6,)),

time: 41.9 us -> 40.9 us (0.976)
  Pallas kernels: 41.1 us -> 40 us
    pallas_call x1, Pallas kernels: 41.1 us -> 40 us  [per_device(): pl.pallas_call(functools.partial(kernel, sizes), out_shape=jax.ShapeDtype...]
where the time goes in v4:
time: 40.9 us; the launch traced here: 40.8 us
  Pallas kernels  40 us (98%)
  local copies, waits for them, and re-layouts  0.75 us (2%)
    pallas_call x1, Pallas kernels, per_device(): pl.pallas_call(functools.partial(kernel, sizes), out_shape=jax.ShapeDtype...  40 us

profile of v4, /device:TPU:8, one launch (start us, length us, event | category | flops | bytes accessed | tf_op | source)
XLA Modules:
  0.0 40.8 jit_solution(10509798914160076222)
XLA Ops:
  0.0 40.0 %hybrid_row.1 = f32[1,6,8,16,128]{4,3,2,1,0:T(8,128)S(1)} custom-call(s32[9]{0:T(128)} %offsets_hbm.1, f32[6,8,6]{2,1,0:T(8,128)} %bitcast.1, f32[1,6,8,16,128]{4,3,2,1,0:T(8,128)} %state_hbm.1, f32[1,6,8,16,128]{4,3,2,1,0:T(8,128)} %mult_hbm.1, bf16[1,40,6,8,16,128]{5,4,3,2,1,0:T(8,128)(2,1)} %mem_hbm.1, f32[1,6,8,16,128]{4,3,2,1,0:T(8,128)} %var_hbm.1, ...), custom_call_target="tpu_custom_call" | custom-call | tf_op jit(solution)/shard_map/hybrid_row/pallas_call | solution.py:579
  40.0 0.7 %copy.9 = f32[1,6,8,16,128]{4,3,2,1,0:T(8,128)} copy(f32[1,6,8,16,128]{4,3,2,1,0:T(8,128)S(1)} %hybrid_row.1) | data formatting | bytes 786432

commit v5 on v4

--- a/solution.py
+++ b/solution.py
@@ -309,13 +309,19 @@
     wind_edge[0] = wind[:, :, 8 + width - 1]
     wind_edge[1] = wind[:, :, 8]
 
-    for h in range(2):
-        edge_copy(h).start()
-        wind_copy(h).start()
+    def start_edges():
+        for h in range(2):
+            edge_copy(h).start()
+            wind_copy(h).start()
+
+    pl.when(~wrap)(start_edges)
     for v in range(1, half):
         load_own(v).wait()
         load_own(half + v).wait()
-        lax.fori_loop(per_var * v, per_var * (v + 1), start_members, 0)
+        lax.fori_loop(per_var * v, min(per_var * (v + 1), last), start_members, 0)
+
+    pl.when(wrap)(start_edges)
+    start_members(last, 0)
 
     @pl.when(wrap)
     def _():

time: 40.9 us -> 40.9 us (level)
  no operation moved by 1% of the time
where the time goes in v5:
time: 40.9 us; the launch traced here: 40.8 us
  Pallas kernels  40 us (98%)
  local copies, waits for them, and re-layouts  0.75 us (2%)
    pallas_call x1, Pallas kernels, per_device(): pl.pallas_call(functools.partial(kernel, sizes), out_shape=jax.ShapeDtype...  40 us

profile of v5, /device:TPU:8, one launch (start us, length us, event | category | flops | bytes accessed | tf_op | source)
XLA Modules:
  0.0 40.8 jit_solution(5012935128291277117)
XLA Ops:
  0.0 40.0 %hybrid_row.1 = f32[1,6,8,16,128]{4,3,2,1,0:T(8,128)S(1)} custom-call(s32[9]{0:T(128)} %offsets_hbm.1, f32[6,8,6]{2,1,0:T(8,128)} %bitcast.1, f32[1,6,8,16,128]{4,3,2,1,0:T(8,128)} %state_hbm.1, f32[1,6,8,16,128]{4,3,2,1,0:T(8,128)} %mult_hbm.1, bf16[1,40,6,8,16,128]{5,4,3,2,1,0:T(8,128)(2,1)} %mem_hbm.1, f32[1,6,8,16,128]{4,3,2,1,0:T(8,128)} %var_hbm.1, ...), custom_call_target="tpu_custom_call" | custom-call | tf_op jit(solution)/shard_map/hybrid_row/pallas_call | solution.py:585
  40.0 0.7 %copy.9 = f32[1,6,8,16,128]{4,3,2,1,0:T(8,128)} copy(f32[1,6,8,16,128]{4,3,2,1,0:T(8,128)S(1)} %hybrid_row.1) | data formatting | bytes 786432
